TPU v7x, 32 devices: a whole 2x2x4 slice. The times are simulated.
32 devices in a mesh: dp: 4 (over y, x), expert: 8 (over z, core).
Axes of the slice: x: 2, y: 2, z: 4, core: 2. Of those that a mesh axis runs over, the one named last changes fastest.
Arguments:
- tokens: bfloat16 [4096, 2048], P(('dp', 'expert')), may hold values from -6 to 6
- expert_ids: int32 [4096, 2], P(('dp', 'expert')), may hold values from 0 to 7, all different within a row; in each aligned block of 128 rows (0 to 127, 128 to 255, ...) at most 40 rows name the same one
- gate_units: int32 [4096, 2], P(('dp', 'expert')), may hold values from 64 to 1023
- capacity: int32 [8], replicated, may hold values from 512 to 1535
- w_gate: bfloat16 [8, 2048, 1408], P('expert', None, 'dp'), may hold values from -0.125 to 0.125
- w_up: bfloat16 [8, 2048, 1408], P('expert', None, 'dp'), may hold values from -0.125 to 0.125
- w_down: bfloat16 [8, 2048, 1408], P('expert', None, 'dp'), may hold values from -0.15625 to 0.15625
Outputs:
- mixed: bfloat16 [4096, 2048], P(('dp', 'expert'))
Inputs may be any that keep to these rules, and one draw needn't show every extreme that they name: `expert_ids`: each row names two different experts; of one device's 128 rows (aligned blocks) no expert is named more than 40 times.
All inputs are finite; a program needn't handle non-finite values.
Results may differ from a plain program's by a relative error of at most 0.0057.
Values may be sent and summed in bfloat16 or wider, within the bound.
No kernel may reach another device: no remote copies, remote signals or barrier semaphores. Data moves between devices by JAX's collectives and lax.ppermute only.
A program may use at most 128 MiB of HBM per device.

v0:
```python
import jax
import jax.numpy as jnp
from jax import lax
from jax.sharding import PartitionSpec as P


def prefix(shard, axis, combine, identity):
    length, here = (lax.axis_size(axis), lax.axis_index(axis))
    everything = lax.all_gather(shard, axis)
    start = jnp.broadcast_to(jnp.asarray(identity, shard.dtype), shard.shape)

    def step(k, before):
        reached = k < here
        new = combine(before, everything[k])
        return jnp.where(reached, new, before)

    return lax.fori_loop(0, length, step, start)


def expert_rows(rows, gate_w, up_w, down_w):
    gate = jnp.dot(rows, gate_w, preferred_element_type=jnp.float32)
    up = jnp.dot(rows, up_w, preferred_element_type=jnp.float32)
    hidden = (jax.nn.silu(gate) * up).astype(jnp.bfloat16)
    return lax.dot_general(
        hidden, down_w, (((1,), (1,)), ((), ())), preferred_element_type=jnp.float32
    )


def add_counts(earlier, later):
    return earlier + later


def local(tokens, expert_ids, gate_units, capacity, w_gate, w_up, w_down):
    tok_rows = tokens.shape[0]
    width = tokens.shape[1]
    n_experts = capacity.shape[0]
    most = max(2, 5 * tok_rows // (2 * n_experts))
    slots_all = n_experts * most
    flat = expert_ids.reshape(-1)
    onehot = (flat[:, None] == jnp.arange(n_experts, dtype=jnp.int32)[None, :]).astype(jnp.int32)
    local_rank = jnp.sum((jnp.cumsum(onehot, axis=0) - onehot) * onehot, axis=1)
    counts = jnp.sum(onehot, axis=0)
    offsets = prefix(counts, ("dp", "expert"), add_counts, jnp.zeros_like(counts))
    global_slot = jnp.sum(onehot * offsets[None, :], axis=1) + local_rank
    limit = jnp.sum(onehot * capacity[None, :], axis=1)
    kept = global_slot < limit
    weight = jnp.where(kept, gate_units.reshape(-1).astype(jnp.float32) / 1024.0, jnp.float32(0.0))
    send_slot = flat * most + local_rank
    chosen = (send_slot[None, :] == jnp.arange(slots_all, dtype=jnp.int32)[:, None]) & kept[None, :]
    placing = jnp.sum(chosen.reshape(slots_all, tok_rows, 2).astype(jnp.int32), axis=2).astype(
        jnp.bfloat16
    )
    outgoing = jnp.dot(placing, tokens, preferred_element_type=jnp.float32).astype(jnp.bfloat16)
    outgoing = outgoing.reshape(n_experts, most, width)
    arrived = lax.all_to_all(outgoing, "expert", split_axis=0, concat_axis=0, tiled=True).reshape(
        slots_all, width
    )
    produced = expert_rows(
        arrived,
        lax.all_gather(w_gate, "dp", axis=2, tiled=True)[0],
        lax.all_gather(w_up, "dp", axis=2, tiled=True)[0],
        lax.all_gather(w_down, "dp", axis=2, tiled=True)[0],
    )
    answer = produced.astype(jnp.bfloat16).reshape(n_experts, most, width)
    back = lax.all_to_all(answer, "expert", split_axis=0, concat_axis=0, tiled=True).reshape(
        slots_all, width
    )
    picked = back[send_slot].astype(jnp.float32) * weight[:, None]
    mixed = jnp.sum(picked.reshape(tok_rows, 2, width), axis=1)
    return mixed.astype(jnp.bfloat16)


def solution(mesh):
    return jax.shard_map(
        local,
        mesh=mesh,
        in_specs=(
            P(("dp", "expert"), None),
            P(("dp", "expert"), None),
            P(("dp", "expert"), None),
            P(),
            P("expert", None, "dp"),
            P("expert", None, "dp"),
            P("expert", None, "dp"),
        ),
        out_specs=P(("dp", "expert"), None),
        check_vma=False,
    )
```

profile of v0, /device:TPU:0, one launch (start us, length us, event | category | flops | bytes accessed | tf_op | source)
XLA Modules:
  0.0 275.7 jit_solution(2728513415111079550)
XLA Ops:
  6.5 0.0 copy-start
  6.5 0.0 all-gather.5.cloned.1.call-start
  6.5 0.7 all-gather.5.cloned.1.call-update
  7.3 0.0 copy-start.1
  7.3 0.0 copy-start.3
  7.3 0.0 copy-start.2
  7.3 0.0 all-gather.7.cloned.1.call-start
  7.3 0.7 all-gather.7.cloned.1.call-update
  8.0 0.0 all-gather.9.cloned.1.call-start
  8.1 0.7 all-gather.9.cloned.1.call-update
  8.8 0.0 copy-done.1
  8.8 0.1 copy.23
  8.9 0.1 eq.39
  9.1 0.1 eq.43
  9.2 0.1 convert_reduce_fusion.1
  9.3 0.2 dynamic-update-slice
  9.6 42.6 %all-reduce = s32[256]{0:T(256)S(1)} all-reduce(s32[256]{0:T(256)S(1)} %dynamic-update-slice), channel_id=2, replica_groups=mesh['dp'=4,'expert'=8] {'dp','expert'}, use_global_device_ids=true, to_apply=%add | all-reduce | flops 256 | bytes 2048
  52.1 0.1 reshape.134
  52.2 0.6 reduce-window.6
  52.8 0.2 slice_reduce_fusion
  53.1 1.3 while.14
  54.4 0.0 copy-done.3
  54.4 0.1 select_reduce_fusion.1
  54.5 0.1 reduce_sum.63
  54.6 0.1 copy.28
  54.7 0.2 reduce_sum.66
  54.8 0.1 copy.27
  54.9 0.2 reduce_sum.68
  55.1 0.1 copy.29
  55.2 0.1 copy.26
  55.2 0.0 copy-done.2
  55.3 0.0 copy-done
  55.3 0.5 convolution_convert_fusion
  55.8 35.6 %all_to_all.10 = bf16[8,40,2048]{2,1,0:T(8,128)(2,1)S(1)} all-to-all(bf16[8,40,2048]{2,1,0:T(8,128)(2,1)S(1)} %bitcast.35), channel_id=1, replica_groups=mesh['dp'=4,'expert'=8] {'expert'}, dimensions={0} | all-to-all | bytes 2621440 | tf_op jit(solution)/shard_map/all_to_all | solution.py:55
  91.4 0.0 all-gather.5.cloned.1.call-done
  91.4 6.1 %fusion.4 = f32[320,1408]{1,0:T(8,128)} fusion(bf16[320,2048]{1,0:T(8,128)(2,1)S(1)} %bitcast.36, bf16[1,2048,1408]{1,2,0:T(8,128)(2,1)} %all-gather.5.cloned.1.call-done), kind=kOutput, calls=%fused_computation.7 | convolution fusion | flops 1845493760 | bytes 8880128 | tf_op jit(solution)/shard_map/dot_general | solution.py:21
  97.5 48.3 %all-gather.7.cloned.1.call-done = bf16[1,2048,1408]{1,2,0:T(8,128)(2,1)} async-done(((bf16[1,2048,352]{1,2,0:T(8,128)(2,1)}), bf16[1,2048,1408]{1,2,0:T(8,128)(2,1)}) %all-gather.7.cloned.1.call-update) | async-done | bytes 5767184 | tf_op jit(solution)/shard_map/all_gather | solution.py:61
  145.8 67.5 %all-gather.9.cloned.1.call-done = bf16[1,2048,1408]{1,2,0:T(8,128)(2,1)} async-done(((bf16[1,2048,352]{1,2,0:T(8,128)(2,1)}), bf16[1,2048,1408]{1,2,0:T(8,128)(2,1)}) %all-gather.9.cloned.1.call-update) | async-done | bytes 5767184 | tf_op jit(solution)/shard_map/all_gather | solution.py:62
  213.4 10.3 %fusion.9 = bf16[320,2048]{1,0:T(8,128)(2,1)} fusion(bf16[1,2048,1408]{1,2,0:T(8,128)(2,1)} %all-gather.9.cloned.1.call-done, bf16[320,2048]{1,0:T(8,128)(2,1)S(1)} %bitcast.37, bf16[1,2048,1408]{1,2,0:T(8,128)(2,1)} %all-gather.7.cloned.1.call-done, f32[320,1408]{1,0:T(8,128)} %fusion.4), kind=kOutput, calls=%fused_computation.10 | convolution fusion | flops 3694346240 | bytes 15958016 | tf_op jit(solution)/shard_map/dot_general | solution.py:24
  223.7 4.6 %all-to-all-start.1 = ((bf16[8,40,2048]{2,1,0:T(8,128)(2,1)}), bf16[8,40,2048]{2,1,0:T(8,128)(2,1)S(1)}, u32[]{:S(2)}, u32[]{:S(2)}) async-start(bf16[8,40,2048]{2,1,0:T(8,128)(2,1)} %bitcast.7), calls=%async_computation.1 | async-start | bytes 2621440 | tf_op jit(solution)/shard_map/all_to_all | solution.py:65
  228.3 0.1 mul.68
  228.4 0.1 copy.30
  228.5 31.9 %all-to-all-done.1 = bf16[8,40,2048]{2,1,0:T(8,128)(2,1)S(1)} async-done(((bf16[8,40,2048]{2,1,0:T(8,128)(2,1)}), bf16[8,40,2048]{2,1,0:T(8,128)(2,1)S(1)}, u32[]{:S(2)}, u32[]{:S(2)}) %all-to-all-start.1) | async-done | bytes 1310752 | tf_op jit(solution)/shard_map/all_to_all | solution.py:65
  260.5 2.3 gather_fusion
  262.8 2.4 reshape.125
  265.2 4.0 %multiply_reduce_fusion = bf16[128,2048]{1,0:T(8,128)(2,1)} fusion(f32[128,2,2048]{2,1,0:T(2,128)S(1)} %reshape.125, f32[128,2]{1,0:T(8,128)S(1)} %copy.30), kind=kLoop, calls=%fused_computation.13 | loop fusion | flops 786432 | bytes 2622464 | tf_op jit(solution)/shard_map/reduce_sum | solution.py:69
  (42 shorter events, 0.7 us)
Async XLA Ops:
  6.5 48.8 %copy-start = (bf16[128,2048]{1,0:T(8,128)(2,1)S(1)}, bf16[128,2048]{1,0:T(8,128)(2,1)}, u32[]{:S(2)}) copy-start(bf16[128,2048]{1,0:T(8,128)(2,1)} %param.9) | copy-start | bytes 1572868
  6.5 84.9 %all-gather.5.cloned.1.call-start = ((), (), s32[]{:S(2)}) async-start(), calls=%async_computation.2 | async-start | bytes 7208960 | tf_op jit(solution)/shard_map/all_gather | solution.py:60
  7.3 1.5 copy-start.1
  7.3 47.1 %copy-start.3 = (s32[8]{0:T(128)S(1)}, s32[8]{0:T(128)}, u32[]{:S(2)}) copy-start(s32[8]{0:T(128)} %param.12) | copy-start | bytes 100
  7.3 47.9 %copy-start.2 = (s32[128,2]{0,1:T(2,128)S(1)}, s32[128,2]{0,1:T(2,128)}, u32[]{:S(2)}) copy-start(s32[128,2]{0,1:T(2,128)} %param.11) | copy-start | bytes 3076
  7.3 138.6 %all-gather.7.cloned.1.call-start = ((), (), s32[]{:S(2)}) async-start(), calls=%async_computation.3 | async-start | bytes 7208960 | tf_op jit(solution)/shard_map/all_gather | solution.py:61
  8.0 205.4 %all-gather.9.cloned.1.call-start = ((), (), s32[]{:S(2)}) async-start(), calls=%async_computation.4 | async-start | bytes 7208960 | tf_op jit(solution)/shard_map/all_gather | solution.py:62
  223.7 36.8 %all-to-all-start.1 = ((bf16[8,40,2048]{2,1,0:T(8,128)(2,1)}), bf16[8,40,2048]{2,1,0:T(8,128)(2,1)S(1)}, u32[]{:S(2)}, u32[]{:S(2)}) async-start(bf16[8,40,2048]{2,1,0:T(8,128)(2,1)} %bitcast.7), calls=%async_computation.1 | async-start | bytes 2621440 | tf_op jit(solution)/shard_map/all_to_all | solution.py:65
Sparse Core Ops, SparseCore 0:
  9.2 69.0 all-gather.4
  80.1 65.6 all-gather.6
  147.7 65.6 all-gather.8
where the time goes:
time: 276 us
  waiting for transfers between devices  150 us (54%)
  blocking collectives  78.1 us (28%)
  matrix products  16.9 us (6%)
  between operations  13.3 us (5%)
  local copies, waits for them, and re-layouts  6.6 us (2%)
  other arithmetic  5.55 us (2%)
  starting transfers between devices  4.68 us (2%)
    all_gather x1, waiting for transfers between devices, local(): lax.all_gather(w_down, 'dp', axis=2, tiled=True)[0]  67.5 us
    all_gather x1, waiting for transfers between devices, local(): lax.all_gather(w_up, 'dp', axis=2, tiled=True)[0]  48.3 us
    unnamed x1, blocking collectives  42.6 us
    all_to_all x1, blocking collectives, local(): lax.all_to_all(outgoing, 'expert', split_axis=0, concat_axis=0, tiled=True)  35.6 us
    all_to_all x1, waiting for transfers between devices, local(): lax.all_to_all(answer, 'expert', split_axis=0, concat_axis=0, tiled=True)  31.9 us
    dot_general x1, matrix products, expert_rows(): lax.dot_general(hidden, down_w, (((1,), (1,)), ((), ())), preferred_eleme...  10.3 us
    dot_general x1, matrix products, expert_rows(): gate = jnp.dot(rows, gate_w, preferred_element_type=jnp.float32)  6.11 us
  transfers between devices with their start and end apart: 4, of which 3 were waited for; matrix products, arithmetic and copies ran while one was open for 4% of the time, Pallas kernels for 0%

commit v1 on v0

--- a/solution.py
+++ b/solution.py
@@ -59,7 +59,7 @@
         arrived,
         lax.all_gather(w_gate, "dp", axis=2, tiled=True)[0],
         lax.all_gather(w_up, "dp", axis=2, tiled=True)[0],
-        lax.all_gather(w_down, "dp", axis=2, tiled=True)[0],
+        jnp.concatenate(lax.all_gather(w_down, "dp"), axis=2)[0],
     )
     answer = produced.astype(jnp.bfloat16).reshape(n_experts, most, width)
     back = lax.all_to_all(answer, "expert", split_axis=0, concat_axis=0, tiled=True).reshape(

time: 276 us -> 276 us (level)
  no operation moved by 1% of the time
where the time goes in v1:
time: 276 us
  waiting for transfers between devices  150 us (54%)
  blocking collectives  78.1 us (28%)
  matrix products  16.9 us (6%)
  between operations  13.3 us (5%)
  local copies, waits for them, and re-layouts  6.6 us (2%)
  other arithmetic  5.55 us (2%)
  starting transfers between devices  4.68 us (2%)
    all_gather x1, waiting for transfers between devices, local(): lax.all_gather(w_down, 'dp')  67.5 us
    all_gather x1, waiting for transfers between devices, local(): lax.all_gather(w_up, 'dp', axis=2, tiled=True)[0]  48.3 us
    unnamed x1, blocking collectives  42.6 us
    all_to_all x1, blocking collectives, local(): lax.all_to_all(outgoing, 'expert', split_axis=0, concat_axis=0, tiled=True)  35.6 us
    all_to_all x1, waiting for transfers between devices, local(): lax.all_to_all(answer, 'expert', split_axis=0, concat_axis=0, tiled=True)  31.9 us
    dot_general x1, matrix products, expert_rows(): lax.dot_general(hidden, down_w, (((1,), (1,)), ((), ())), preferred_eleme...  10.3 us
    dot_general x1, matrix products, expert_rows(): gate = jnp.dot(rows, gate_w, preferred_element_type=jnp.float32)  6.11 us
  transfers between devices with their start and end apart: 4, of which 3 were waited for; matrix products, arithmetic and copies ran while one was open for 4% of the time, Pallas kernels for 0%

profile of v1, /device:TPU:0, one launch (start us, length us, event | category | flops | bytes accessed | tf_op | source)
XLA Modules:
  0.0 275.7 jit_solution(5200091513108538925)
XLA Ops:
  6.5 0.0 copy-start
  6.5 0.0 all-gather.6.cloned.1.call-start
  6.5 0.7 all-gather.6.cloned.1.call-update
  7.3 0.0 copy-start.1
  7.3 0.0 copy-start.3
  7.3 0.0 copy-start.2
  7.3 0.0 all-gather.8.cloned.1.call-start
  7.3 0.7 all-gather.8.cloned.1.call-update
  8.0 0.0 all-gather.10.cloned.1.call-start
  8.1 0.7 all-gather.10.cloned.1.call-update
  8.8 0.0 copy-done.1
  8.8 0.1 copy.28
  8.9 0.1 eq.39
  9.1 0.1 eq.43
  9.2 0.1 convert_reduce_fusion.1
  9.3 0.2 dynamic-update-slice
  9.6 42.6 %all-reduce = s32[256]{0:T(256)S(1)} all-reduce(s32[256]{0:T(256)S(1)} %dynamic-update-slice), channel_id=2, replica_groups=mesh['dp'=4,'expert'=8] {'dp','expert'}, use_global_device_ids=true, to_apply=%add | all-reduce | flops 256 | bytes 2048
  52.1 0.1 reshape.138
  52.2 0.6 reduce-window.6
  52.8 0.2 slice_reduce_fusion
  53.1 1.3 while.14
  54.4 0.0 copy-done.3
  54.4 0.1 select_reduce_fusion.1
  54.5 0.1 reduce_sum.63
  54.6 0.1 copy.33
  54.7 0.2 reduce_sum.66
  54.8 0.1 copy.32
  54.9 0.2 reduce_sum.68
  55.1 0.1 copy.34
  55.2 0.1 copy.31
  55.2 0.0 copy-done.2
  55.3 0.0 copy-done
  55.3 0.5 convolution_convert_fusion.1
  55.8 35.6 %all_to_all.10 = bf16[8,40,2048]{2,1,0:T(8,128)(2,1)S(1)} all-to-all(bf16[8,40,2048]{2,1,0:T(8,128)(2,1)S(1)} %bitcast.36), channel_id=1, replica_groups=mesh['dp'=4,'expert'=8] {'expert'}, dimensions={0} | all-to-all | bytes 2621440 | tf_op jit(solution)/shard_map/all_to_all | solution.py:55
  91.4 0.0 all-gather.6.cloned.1.call-done
  91.4 6.1 %fusion.2 = f32[320,1408]{1,0:T(8,128)} fusion(bf16[320,2048]{1,0:T(8,128)(2,1)S(1)} %bitcast.37, bf16[1,2048,1408]{1,2,0:T(8,128)(2,1)} %all-gather.6.cloned.1.call-done), kind=kOutput, calls=%fused_computation.5 | convolution fusion | flops 1845493760 | bytes 8880128 | tf_op jit(solution)/shard_map/dot_general | solution.py:21
  97.5 48.3 %all-gather.8.cloned.1.call-done = bf16[1,2048,1408]{1,2,0:T(8,128)(2,1)} async-done(((bf16[1,2048,352]{1,2,0:T(8,128)(2,1)}), bf16[1,2048,1408]{1,2,0:T(8,128)(2,1)}) %all-gather.8.cloned.1.call-update) | async-done | bytes 5767184 | tf_op jit(solution)/shard_map/all_gather | solution.py:61
  145.8 67.5 %all-gather.10.cloned.1.call-done = bf16[4,2048,352]{1,2,0:T(8,128)(2,1)} async-done(((bf16[1,2048,352]{1,2,0:T(8,128)(2,1)}), bf16[4,2048,352]{1,2,0:T(8,128)(2,1)}) %all-gather.10.cloned.1.call-update) | async-done | bytes 5767184 | tf_op jit(solution)/shard_map/all_gather | solution.py:62
  213.4 10.3 %convolution_convert_fusion = bf16[320,2048]{1,0:T(8,128)(2,1)} fusion(bf16[2048,1408]{0,1:T(8,128)(2,1)} %bitcast.41, bf16[320,2048]{1,0:T(8,128)(2,1)S(1)} %bitcast.38, bf16[1,2048,1408]{1,2,0:T(8,128)(2,1)} %all-gather.8.cloned.1.call-done, f32[320,1408]{1,0:T(8,128)} %fusion.2), kind=kOutput, calls=%fused_computation.8 | convolution fusion | flops 3694346240 | bytes 15958016 | tf_op jit(solution)/shard_map/dot_general | solution.py:24
  223.7 4.6 %all-to-all-start.1 = ((bf16[8,40,2048]{2,1,0:T(8,128)(2,1)}), bf16[8,40,2048]{2,1,0:T(8,128)(2,1)S(1)}, u32[]{:S(2)}, u32[]{:S(2)}) async-start(bf16[8,40,2048]{2,1,0:T(8,128)(2,1)} %bitcast.9), calls=%async_computation.1 | async-start | bytes 2621440 | tf_op jit(solution)/shard_map/all_to_all | solution.py:65
  228.3 0.1 mul.68
  228.4 0.1 copy.35
  228.5 31.9 %all-to-all-done.1 = bf16[8,40,2048]{2,1,0:T(8,128)(2,1)S(1)} async-done(((bf16[8,40,2048]{2,1,0:T(8,128)(2,1)}), bf16[8,40,2048]{2,1,0:T(8,128)(2,1)S(1)}, u32[]{:S(2)}, u32[]{:S(2)}) %all-to-all-start.1) | async-done | bytes 1310752 | tf_op jit(solution)/shard_map/all_to_all | solution.py:65
  260.5 2.3 gather_fusion
  262.8 2.4 reshape.129
  265.2 4.0 %multiply_reduce_fusion = bf16[128,2048]{1,0:T(8,128)(2,1)} fusion(f32[128,2,2048]{2,1,0:T(2,128)S(1)} %reshape.129, f32[128,2]{1,0:T(8,128)S(1)} %copy.35), kind=kLoop, calls=%fused_computation.11 | loop fusion | flops 786432 | bytes 2622464 | tf_op jit(solution)/shard_map/reduce_sum | solution.py:69
  (42 shorter events, 0.7 us)
Async XLA Ops:
  6.5 48.8 %copy-start = (bf16[128,2048]{1,0:T(8,128)(2,1)S(1)}, bf16[128,2048]{1,0:T(8,128)(2,1)}, u32[]{:S(2)}) copy-start(bf16[128,2048]{1,0:T(8,128)(2,1)} %param.9) | copy-start | bytes 1572868
  6.5 84.9 %all-gather.6.cloned.1.call-start = ((), (), s32[]{:S(2)}) async-start(), calls=%async_computation.2 | async-start | bytes 7208960 | tf_op jit(solution)/shard_map/all_gather | solution.py:60
  7.3 1.5 copy-start.1
  7.3 47.1 %copy-start.3 = (s32[8]{0:T(128)S(1)}, s32[8]{0:T(128)}, u32[]{:S(2)}) copy-start(s32[8]{0:T(128)} %param.12) | copy-start | bytes 100
  7.3 47.9 %copy-start.2 = (s32[128,2]{0,1:T(2,128)S(1)}, s32[128,2]{0,1:T(2,128)}, u32[]{:S(2)}) copy-start(s32[128,2]{0,1:T(2,128)} %param.11) | copy-start | bytes 3076
  7.3 138.6 %all-gather.8.cloned.1.call-start = ((), (), s32[]{:S(2)}) async-start(), calls=%async_computation.3 | async-start | bytes 7208960 | tf_op jit(solution)/shard_map/all_gather | solution.py:61
  8.0 205.4 %all-gather.10.cloned.1.call-start = ((), (), s32[]{:S(2)}) async-start(), calls=%async_computation.4 | async-start | bytes 7208960 | tf_op jit(solution)/shard_map/all_gather | solution.py:62
  223.7 36.8 %all-to-all-start.1 = ((bf16[8,40,2048]{2,1,0:T(8,128)(2,1)}), bf16[8,40,2048]{2,1,0:T(8,128)(2,1)S(1)}, u32[]{:S(2)}, u32[]{:S(2)}) async-start(bf16[8,40,2048]{2,1,0:T(8,128)(2,1)} %bitcast.9), calls=%async_computation.1 | async-start | bytes 2621440 | tf_op jit(solution)/shard_map/all_to_all | solution.py:65
Sparse Core Ops, SparseCore 0:
  9.2 69.0 all-gather.5
  80.1 65.6 all-gather.7
  147.7 65.6 all-gather.9
